TPU v7x, 32 devices: a whole 2x2x4 slice. The times are simulated.
32 devices in a mesh: row: 8 (over y, x, core), col: 4 (over z).
Axes of the slice: x: 2, y: 2, z: 4, core: 2. Of those that a mesh axis runs over, the one named last changes fastest.
Arguments:
- field: float32 [64, 128, 512], P(None, 'row', 'col'), may hold values from -4 to 6.5, as said below
- conductivity: float32 [64, 128, 512], P(None, 'row', 'col'), may hold values from 35 to 5600, as said below
Outputs:
- new_field: float32 [64, 128, 512], P(None, 'row', 'col')
Inputs may be any that keep to these rules, and one draw needn't show every extreme that they name: `field`: finite values. `conductivity`: positive in every cell.
All inputs are finite; a program needn't handle non-finite values.
Results may differ from a plain program's by a relative error of at most 0.0003.
Values sent between devices are 32-bit elements; how exact they have to be, the bound alone decides.
A program may use at most 64 MiB of HBM per device.

v0:
```python
import jax
import jax.numpy as jnp
from jax import lax
from jax.sharding import PartitionSpec as P

z_weight = 0.02


def padded_2(block, sides, width):
    for axis, dim in sides:
        count = lax.axis_size(axis)
        forward = [(i, i + 1) for i in range(count - 1)]
        backward = [(target, source) for source, target in forward]
        low = lax.ppermute(
            lax.slice_in_dim(block, block.shape[dim] - width, None, axis=dim), axis, forward
        )
        high = lax.ppermute(lax.slice_in_dim(block, 0, width, axis=dim), axis, backward)
        block = jnp.concatenate([low, block, high], axis=dim)
    return block


def neighbour(values, line_axis, offset):
    length = values.shape[line_axis]
    widths = [(0, 0)] * values.ndim
    widths[line_axis] = (1, 1)
    padded = jnp.pad(values, widths)
    return lax.slice_in_dim(padded, 1 + offset, 1 + offset + length, axis=line_axis)


def shifted(values, line_axis, stride, fill):
    length = values.shape[line_axis]
    pad_shape = list(values.shape)
    pad_shape[line_axis] = abs(stride)
    padding = jnp.full(pad_shape, fill, values.dtype)
    if stride > 0:
        kept_part = lax.slice_in_dim(values, 0, length - stride, axis=line_axis)
        return jnp.concatenate((padding, kept_part), axis=line_axis)
    kept_part = lax.slice_in_dim(values, -stride, length, axis=line_axis)
    return jnp.concatenate((kept_part, padding), axis=line_axis)


def reduce_lines(below_diag, diagonal, above_diag, columns, line_axis):
    length = diagonal.shape[line_axis]
    stride = 1
    while stride < length:
        left_factor = -below_diag / shifted(diagonal, line_axis, stride, 1.0)
        right_factor = -above_diag / shifted(diagonal, line_axis, -stride, 1.0)
        new_diag = (
            diagonal
            + left_factor * shifted(above_diag, line_axis, stride, 0.0)
            + right_factor * shifted(below_diag, line_axis, -stride, 0.0)
        )
        new_below = left_factor * shifted(below_diag, line_axis, stride, 0.0)
        new_above = right_factor * shifted(above_diag, line_axis, -stride, 0.0)
        columns = [
            column
            + left_factor * shifted(column, line_axis, stride, 0.0)
            + right_factor * shifted(column, line_axis, -stride, 0.0)
            for column in columns
        ]
        below_diag, diagonal, above_diag = (new_below, new_diag, new_above)
        stride = stride * 2
    return (diagonal, columns)


def local_spikes(below_diag, above_diag, right_side, line_axis):
    length = right_side.shape[line_axis]
    position = lax.broadcasted_iota(jnp.int32, right_side.shape, line_axis)
    first_row = position == 0
    last_row = position == length - 1
    diagonal = 1.0 - below_diag - above_diag
    left_column = jnp.where(first_row, below_diag, 0.0)
    right_column = jnp.where(last_row, above_diag, 0.0)
    below_inner = jnp.where(first_row, 0.0, below_diag)
    above_inner = jnp.where(last_row, 0.0, above_diag)
    diagonal, columns = reduce_lines(
        below_inner, diagonal, above_inner, [right_side, left_column, right_column], line_axis
    )
    local_part = columns[0] / diagonal
    left_spike = columns[1] / diagonal
    right_spike = columns[2] / diagonal
    planes = []
    for member in (local_part, left_spike, right_spike):
        planes.append(lax.index_in_dim(member, 0, line_axis, keepdims=False))
        planes.append(lax.index_in_dim(member, length - 1, line_axis, keepdims=False))
    return (local_part, left_spike, right_spike, jnp.stack(planes)[None])


def join_spikes(gathered, local_part, left_spike, right_spike, line_axis, index_here, group_size):
    columns_in = tuple((gathered[:, member] for member in range(6)))
    zero_plane = jnp.zeros_like(columns_in[0][0])

    def forward(state_now, inputs):
        spike_prev, carry_prev = state_now
        head_local, tail_local, head_left, tail_left, head_right, tail_right = inputs
        pivot_here = 1.0 - head_left * spike_prev
        ratio_here = head_right / pivot_here
        first_here = (head_local - head_left * carry_prev) / pivot_here
        spike_next = tail_right + tail_left * spike_prev * ratio_here
        carry_next = tail_local - tail_left * carry_prev + tail_left * spike_prev * first_here
        return ((spike_next, carry_next), (ratio_here, spike_next, first_here, carry_next))

    unused, outputs = lax.scan(forward, (zero_plane, zero_plane), columns_in)

    def backward(next_head, inputs):
        ratio_here, spike_here, first_here, last_here = inputs
        head_value = first_here - ratio_here * next_head
        tail_value = last_here - spike_here * next_head
        return (head_value, (head_value, tail_value))

    unused_last, ends = lax.scan(backward, zero_plane, outputs, reverse=True)
    first_values, last_values = ends
    left_value = lax.dynamic_index_in_dim(
        last_values, jnp.maximum(index_here - 1, 0), 0, keepdims=False
    ) * (index_here > 0).astype(jnp.float32)
    right_value = lax.dynamic_index_in_dim(
        first_values, jnp.minimum(index_here + 1, group_size - 1), 0, keepdims=False
    ) * (index_here < group_size - 1).astype(jnp.float32)
    return (
        local_part
        - jnp.expand_dims(left_value, line_axis) * left_spike
        - jnp.expand_dims(right_value, line_axis) * right_spike
    )


def on_device(field, conductivity):
    stacked = jnp.stack((field, conductivity))
    padded = padded_2(stacked, (("row", 2), ("col", 3)), 1)
    field_pad = padded[0]
    cond_pad = padded[1]
    west_cond = cond_pad[:, :-2, 1:-1]
    east_cond = cond_pad[:, 2:, 1:-1]
    south_cond = cond_pad[:, 1:-1, :-2]
    north_cond = cond_pad[:, 1:-1, 2:]
    west_field = field_pad[:, :-2, 1:-1]
    east_field = field_pad[:, 2:, 1:-1]
    south_field = field_pad[:, 1:-1, :-2]
    north_field = field_pad[:, 1:-1, 2:]
    east_xdir = 0.5 * 1.0 * (conductivity + east_cond)
    west_xdir = 0.5 * 1.0 * (conductivity + west_cond)
    east_ydir = 0.5 * 1.0 * (conductivity + north_cond)
    west_ydir = 0.5 * 1.0 * (conductivity + south_cond)
    flux_xdir = east_xdir * (east_field - field) - west_xdir * (field - west_field)
    flux_ydir = east_ydir * (north_field - field) - west_ydir * (field - south_field)
    east_zdir = 0.5 * z_weight * (conductivity + neighbour(conductivity, 0, 1))
    west_zdir = 0.5 * z_weight * (conductivity + neighbour(conductivity, 0, -1))
    flux_zdir = east_zdir * (neighbour(field, 0, 1) - field) - west_zdir * (
        field - neighbour(field, 0, -1)
    )
    explicit = flux_xdir + flux_ydir + flux_zdir
    local_part, left_spike, right_spike, planes = local_spikes(-west_xdir, -east_xdir, explicit, 1)
    gathered = lax.all_gather(planes, "row", axis=0, tiled=True)
    delta_xdir = join_spikes(
        gathered,
        local_part,
        left_spike,
        right_spike,
        1,
        lax.axis_index("row"),
        lax.axis_size("row"),
    )
    local_part, left_spike, right_spike, planes = local_spikes(
        -west_ydir, -east_ydir, delta_xdir, 2
    )
    gathered = lax.all_gather(planes, "col", axis=0, tiled=True)
    delta_ydir = join_spikes(
        gathered,
        local_part,
        left_spike,
        right_spike,
        2,
        lax.axis_index("col"),
        lax.axis_size("col"),
    )
    return field + delta_ydir


def solution(mesh):
    in_specs = (P(None, "row", "col"), P(None, "row", "col"))
    out_specs = P(None, "row", "col")
    return jax.shard_map(
        on_device, mesh=mesh, in_specs=in_specs, out_specs=out_specs, check_vma=False
    )
```

profile of v0, /device:TPU:0, one launch (start us, length us, event | category | flops | bytes accessed | tf_op | source)
XLA Modules:
  0.0 144.2 jit_solution(15308119017377806291)
XLA Ops:
  6.5 2.5 %fusion.59 = (f32[64,16,128]{2,0,1:T(8,128)}, f32[1,64,16,128]{3,1,2,0:T(8,128)S(1)}, f32[1,64,16,128]{3,1,2,0:T(8,128)S(1)}, f32[64,16,128]{2,0,1:T(8,128)}) fusion(f32[64,16,128]{2,1,0:T(8,128)} %param.10, f32[64,16,128]{2,1,0:T(8,128)} %param.11), kind=kLoop, calls=%fused_computation.241 | loop fusion | bytes 3145728 | tf_op args[0]
  10.4 3.0 %collective-permute-start = (f32[2,64,1,128]{3,1,2,0:T(8,128)S(1)}, f32[2,64,1,128]{3,1,2,0:T(8,128)S(1)}, u32[]{:S(2)}, u32[]{:S(2)}) collective-permute-start(f32[2,64,1,128]{3,1,2,0:T(8,128)S(1)} %get-tuple-element.850), channel_id=1, source_target_pairs={{0,4},{4,8},{8,12},{12,16},{16,20},{20,24},{24,28},{1,5},{5,9},{9,... | collective-permute-start | bytes 196616 | tf_op jit(solution)/shard_map/ppermute | solution.py:14
  17.6 6.2 %collective-permute-start.2 = (f32[2,64,18,1]{1,0,3,2:T(2,128)S(1)}, f32[2,64,18,1]{1,0,3,2:T(2,128)}, u32[]{:S(2)}, u32[]{:S(2)}) collective-permute-start(f32[2,64,18,1]{1,0,3,2:T(2,128)S(1)} %copy.303), channel_id=1, source_target_pairs={{0,1},{1,2},{2,3},{4,5},{5,6},{6,7},{8,9},{9,10},{10,11},{12,13},{... | collective-permute-start | bytes 27656 | tf_op jit(solution)/shard_map/ppermute | solution.py:14
  45.8 23.3 %all-gather.4.cloned.1.call-done = f32[48,64,128]{2,1,0:T(8,128)} async-done(((f32[6,64,128]{2,1,0:T(8,128)}), f32[48,64,128]{2,1,0:T(8,128)}) %all-gather.4.cloned.1.call-update) | async-done | bytes 1572880 | tf_op jit(solution)/shard_map/all_gather | solution.py:152
  69.1 2.4 %slice_bitcast_fusion.2 = (f32[8,64,128]{2,1,0:T(8,128)S(1)}, f32[8,64,128]{2,1,0:T(8,128)S(1)}, f32[8,64,128]{2,1,0:T(8,128)}, f32[8,64,128]{2,1,0:T(8,128)}, f32[8,64,128]{2,1,0:T(8,128)}, /*index=5*/f32[8,64,128]{2,1,0:T(8,128)}) fusion(f32[8,6,64,128]{3,2,1,0:T(8,128)} %bitcast.281), kind=kLoop, calls=%fused_computation.177 | loop fusion | bytes 3145728 | tf_op jit(solution)/shard_map/squeeze | solution.py:90
  74.4 12.1 %while.80 = (s32[]{:T(128)}, f32[64,128]{1,0:T(8,128)S(1)}, f32[64,128]{1,0:T(8,128)S(1)}, f32[8,64,128]{2,1,0:T(8,128)}, f32[8,64,128]{2,1,0:T(8,128)}, /*index...) while((s32[]{:T(128)}, f32[64,128]{1,0:T(8,128)S(1)}, ...), condition=%wide.region_1.2_spmd.clone, body=%wide.region_0.1_spmd.clone.sunk | while | flops 122883 | bytes 458915 | solution.py:103
  74.4 1.6 %bitcast_dynamic-update-slice_fusion.16 = (f32[8,64,128]{2,1,0:T(8,128)}, f32[64,128]{1,0:T(8,128)S(1)}, f32[8,64,128]{2,1,0:T(8,128)}, f32[8,64,128]{2,1,0:T(8,...) fusion(f32[8,64,128]{2,1,0:T(8,128)} %get-tuple-element.1309, s32[]{:T(128)S(6)} %copy.408, ...), kind=kLoop, calls=%fused_computation.clone.1 | loop fusion | flops 122880 | bytes 458757 | tf_op jit(solution)/shard_map/while/body/jit(dynamic_update_index_in_dim)/dynamic_update_slice | solution.py:103
  76.0 1.5 %bitcast_dynamic-update-slice_fusion.16 = (f32[8,64,128]{2,1,0:T(8,128)}, f32[64,128]{1,0:T(8,128)S(1)}, f32[8,64,128]{2,1,0:T(8,128)}, f32[8,64,128]{2,1,0:T(8,...) fusion(f32[8,64,128]{2,1,0:T(8,128)} %get-tuple-element.1309, s32[]{:T(128)S(6)} %copy.408, ...), kind=kLoop, calls=%fused_computation.clone.1 | loop fusion | flops 122880 | bytes 458757 | tf_op jit(solution)/shard_map/while/body/jit(dynamic_update_index_in_dim)/dynamic_update_slice | solution.py:103
  77.5 1.5 %bitcast_dynamic-update-slice_fusion.16 = (f32[8,64,128]{2,1,0:T(8,128)}, f32[64,128]{1,0:T(8,128)S(1)}, f32[8,64,128]{2,1,0:T(8,128)}, f32[8,64,128]{2,1,0:T(8,...) fusion(f32[8,64,128]{2,1,0:T(8,128)} %get-tuple-element.1309, s32[]{:T(128)S(6)} %copy.408, ...), kind=kLoop, calls=%fused_computation.clone.1 | loop fusion | flops 122880 | bytes 458757 | tf_op jit(solution)/shard_map/while/body/jit(dynamic_update_index_in_dim)/dynamic_update_slice | solution.py:103
  79.0 1.5 %bitcast_dynamic-update-slice_fusion.16 = (f32[8,64,128]{2,1,0:T(8,128)}, f32[64,128]{1,0:T(8,128)S(1)}, f32[8,64,128]{2,1,0:T(8,128)}, f32[8,64,128]{2,1,0:T(8,...) fusion(f32[8,64,128]{2,1,0:T(8,128)} %get-tuple-element.1309, s32[]{:T(128)S(6)} %copy.408, ...), kind=kLoop, calls=%fused_computation.clone.1 | loop fusion | flops 122880 | bytes 458757 | tf_op jit(solution)/shard_map/while/body/jit(dynamic_update_index_in_dim)/dynamic_update_slice | solution.py:103
  80.5 1.5 %bitcast_dynamic-update-slice_fusion.16 = (f32[8,64,128]{2,1,0:T(8,128)}, f32[64,128]{1,0:T(8,128)S(1)}, f32[8,64,128]{2,1,0:T(8,128)}, f32[8,64,128]{2,1,0:T(8,...) fusion(f32[8,64,128]{2,1,0:T(8,128)} %get-tuple-element.1309, s32[]{:T(128)S(6)} %copy.408, ...), kind=kLoop, calls=%fused_computation.clone.1 | loop fusion | flops 122880 | bytes 458757 | tf_op jit(solution)/shard_map/while/body/jit(dynamic_update_index_in_dim)/dynamic_update_slice | solution.py:103
  82.0 1.5 %bitcast_dynamic-update-slice_fusion.16 = (f32[8,64,128]{2,1,0:T(8,128)}, f32[64,128]{1,0:T(8,128)S(1)}, f32[8,64,128]{2,1,0:T(8,128)}, f32[8,64,128]{2,1,0:T(8,...) fusion(f32[8,64,128]{2,1,0:T(8,128)} %get-tuple-element.1309, s32[]{:T(128)S(6)} %copy.408, ...), kind=kLoop, calls=%fused_computation.clone.1 | loop fusion | flops 122880 | bytes 458757 | tf_op jit(solution)/shard_map/while/body/jit(dynamic_update_index_in_dim)/dynamic_update_slice | solution.py:103
  83.5 1.5 %bitcast_dynamic-update-slice_fusion.16 = (f32[8,64,128]{2,1,0:T(8,128)}, f32[64,128]{1,0:T(8,128)S(1)}, f32[8,64,128]{2,1,0:T(8,128)}, f32[8,64,128]{2,1,0:T(8,...) fusion(f32[8,64,128]{2,1,0:T(8,128)} %get-tuple-element.1309, s32[]{:T(128)S(6)} %copy.408, ...), kind=kLoop, calls=%fused_computation.clone.1 | loop fusion | flops 122880 | bytes 458757 | tf_op jit(solution)/shard_map/while/body/jit(dynamic_update_index_in_dim)/dynamic_update_slice | solution.py:103
  85.0 1.5 %bitcast_dynamic-update-slice_fusion.16 = (f32[8,64,128]{2,1,0:T(8,128)}, f32[64,128]{1,0:T(8,128)S(1)}, f32[8,64,128]{2,1,0:T(8,128)}, f32[8,64,128]{2,1,0:T(8,...) fusion(f32[8,64,128]{2,1,0:T(8,128)} %get-tuple-element.1309, s32[]{:T(128)S(6)} %copy.408, ...), kind=kLoop, calls=%fused_computation.clone.1 | loop fusion | flops 122880 | bytes 458757 | tf_op jit(solution)/shard_map/while/body/jit(dynamic_update_index_in_dim)/dynamic_update_slice | solution.py:103
  87.9 11.6 %while.81 = (s32[]{:T(128)}, f32[64,128]{1,0:T(8,128)S(1)}, f32[8,64,128]{2,1,0:T(8,128)}, f32[8,64,128]{2,1,0:T(8,128)}, f32[8,64,128]{2,1,0:T(8,128)}, /*index...) while((s32[]{:T(128)}, f32[64,128]{1,0:T(8,128)S(1)}, ...), condition=%wide.region_3.4_spmd.clone, body=%wide.region_2.3_spmd.clone.sunk | while | flops 40964 | bytes 262287 | solution.py:111
  87.9 1.5 %bitcast_dynamic-update-slice_fusion.17 = (f32[8,64,128]{2,1,0:T(8,128)}, f32[64,128]{1,0:T(8,128)S(1)}, f32[8,64,128]{2,1,0:T(8,128)}) fusion(f32[8,64,128]{2,1,0:T(8,128)} %get-tuple-element.1346, s32[]{:T(128)S(6)} %sub.273, f32[64,128]{1,0:T(8,128)S(1)} %get-tuple-element.1345, pred[]{:T(512)S(6)} %compare.143, ...), kind=kLoop, calls=%fused_computation.18.clone.1 | loop fusion | flops 40960 | bytes 262149 | tf_op jit(solution)/shard_map/while/body/jit(dynamic_update_index_in_dim)/dynamic_update_slice | solution.py:103
  90.8 1.5 %bitcast_dynamic-update-slice_fusion.17 = (f32[8,64,128]{2,1,0:T(8,128)}, f32[64,128]{1,0:T(8,128)S(1)}, f32[8,64,128]{2,1,0:T(8,128)}) fusion(f32[8,64,128]{2,1,0:T(8,128)} %get-tuple-element.1346, s32[]{:T(128)S(6)} %sub.273, f32[64,128]{1,0:T(8,128)S(1)} %get-tuple-element.1345, pred[]{:T(512)S(6)} %compare.143, ...), kind=kLoop, calls=%fused_computation.18.clone.1 | loop fusion | flops 40960 | bytes 262149 | tf_op jit(solution)/shard_map/while/body/jit(dynamic_update_index_in_dim)/dynamic_update_slice | solution.py:103
  92.3 1.4 %bitcast_dynamic-update-slice_fusion.17 = (f32[8,64,128]{2,1,0:T(8,128)}, f32[64,128]{1,0:T(8,128)S(1)}, f32[8,64,128]{2,1,0:T(8,128)}) fusion(f32[8,64,128]{2,1,0:T(8,128)} %get-tuple-element.1346, s32[]{:T(128)S(6)} %sub.273, f32[64,128]{1,0:T(8,128)S(1)} %get-tuple-element.1345, pred[]{:T(512)S(6)} %compare.143, ...), kind=kLoop, calls=%fused_computation.18.clone.1 | loop fusion | flops 40960 | bytes 262149 | tf_op jit(solution)/shard_map/while/body/jit(dynamic_update_index_in_dim)/dynamic_update_slice | solution.py:103
  93.7 1.4 %bitcast_dynamic-update-slice_fusion.17 = (f32[8,64,128]{2,1,0:T(8,128)}, f32[64,128]{1,0:T(8,128)S(1)}, f32[8,64,128]{2,1,0:T(8,128)}) fusion(f32[8,64,128]{2,1,0:T(8,128)} %get-tuple-element.1346, s32[]{:T(128)S(6)} %sub.273, f32[64,128]{1,0:T(8,128)S(1)} %get-tuple-element.1345, pred[]{:T(512)S(6)} %compare.143, ...), kind=kLoop, calls=%fused_computation.18.clone.1 | loop fusion | flops 40960 | bytes 262149 | tf_op jit(solution)/shard_map/while/body/jit(dynamic_update_index_in_dim)/dynamic_update_slice | solution.py:103
  95.2 1.5 %bitcast_dynamic-update-slice_fusion.17 = (f32[8,64,128]{2,1,0:T(8,128)}, f32[64,128]{1,0:T(8,128)S(1)}, f32[8,64,128]{2,1,0:T(8,128)}) fusion(f32[8,64,128]{2,1,0:T(8,128)} %get-tuple-element.1346, s32[]{:T(128)S(6)} %sub.273, f32[64,128]{1,0:T(8,128)S(1)} %get-tuple-element.1345, pred[]{:T(512)S(6)} %compare.143, ...), kind=kLoop, calls=%fused_computation.18.clone.1 | loop fusion | flops 40960 | bytes 262149 | tf_op jit(solution)/shard_map/while/body/jit(dynamic_update_index_in_dim)/dynamic_update_slice | solution.py:103
  96.6 1.4 %bitcast_dynamic-update-slice_fusion.17 = (f32[8,64,128]{2,1,0:T(8,128)}, f32[64,128]{1,0:T(8,128)S(1)}, f32[8,64,128]{2,1,0:T(8,128)}) fusion(f32[8,64,128]{2,1,0:T(8,128)} %get-tuple-element.1346, s32[]{:T(128)S(6)} %sub.273, f32[64,128]{1,0:T(8,128)S(1)} %get-tuple-element.1345, pred[]{:T(512)S(6)} %compare.143, ...), kind=kLoop, calls=%fused_computation.18.clone.1 | loop fusion | flops 40960 | bytes 262149 | tf_op jit(solution)/shard_map/while/body/jit(dynamic_update_index_in_dim)/dynamic_update_slice | solution.py:103
  98.1 1.5 %bitcast_dynamic-update-slice_fusion.17 = (f32[8,64,128]{2,1,0:T(8,128)}, f32[64,128]{1,0:T(8,128)S(1)}, f32[8,64,128]{2,1,0:T(8,128)}) fusion(f32[8,64,128]{2,1,0:T(8,128)} %get-tuple-element.1346, s32[]{:T(128)S(6)} %sub.273, f32[64,128]{1,0:T(8,128)S(1)} %get-tuple-element.1345, pred[]{:T(512)S(6)} %compare.143, ...), kind=kLoop, calls=%fused_computation.18.clone.1 | loop fusion | flops 40960 | bytes 262149 | tf_op jit(solution)/shard_map/while/body/jit(dynamic_update_index_in_dim)/dynamic_update_slice | solution.py:103
  103.3 2.1 %multiply_add_fusion.24 = (f32[64,16,128]{2,0,1:T(8,128)S(1)}, f32[64,16,128]{2,0,1:T(8,128)S(1)}, f32[64,16,128]{2,0,1:T(8,128)S(1)}, f32[64,16,128]{2,0,1:T(8,...) fusion(f32[64,16,128]{2,0,1:T(8,128)S(1)} %copy-done.5, ...), kind=kLoop, calls=%fused_computation.141 | loop fusion | flops 2359296 | bytes 11476992 | tf_op jit(solution)/shard_map/add | solution.py:56
  121.5 13.8 %all-gather.1 = f32[24,64,16]{1,2,0:T(8,128)S(1)} all-gather(f32[6,64,16]{1,2,0:T(8,128)S(1)} %constant_dynamic-update-slice_fusion), channel_id=3, replica_groups=mesh['row'=8,'col'=4] {'col'}, dimensions={0}, use_global_device_ids=true | all-gather | bytes 122880 | tf_op jit(solution)/shard_map/all_gather | solution.py:165
  (202 shorter events, 54.5 us)
Async XLA Ops:
  6.5 62.6 %all-gather.4.cloned.1.call-start = ((), (), s32[]{:S(2)}) async-start(), calls=%async_computation | async-start | bytes 1769472 | tf_op jit(solution)/shard_map/all_gather | solution.py:152
  9.1 4.4 %collective-permute-start.1 = (f32[2,64,1,128]{3,1,2,0:T(8,128)S(1)}, f32[2,64,1,128]{3,1,2,0:T(8,128)S(1)}, u32[]{:S(2)}, u32[]{:S(2)}) collective-permute-start(f32[2,64,1,128]{3,1,2,0:T(8,128)S(1)} %get-tuple-element.851), channel_id=1, source_target_pairs={{4,0},{8,4},{12,8},{16,12},{20,16},{24,20},{28,24},{5,1},{9,5},{13... | collective-permute-start | bytes 196616 | tf_op jit(solution)/shard_map/ppermute | solution.py:17
  10.4 3.9 %collective-permute-start = (f32[2,64,1,128]{3,1,2,0:T(8,128)S(1)}, f32[2,64,1,128]{3,1,2,0:T(8,128)S(1)}, u32[]{:S(2)}, u32[]{:S(2)}) collective-permute-start(f32[2,64,1,128]{3,1,2,0:T(8,128)S(1)} %get-tuple-element.850), channel_id=1, source_target_pairs={{0,4},{4,8},{8,12},{12,16},{16,20},{20,24},{24,28},{1,5},{5,9},{9,... | collective-permute-start | bytes 196616 | tf_op jit(solution)/shard_map/ppermute | solution.py:14
  15.9 7.9 %collective-permute-start.3 = (f32[2,64,18,1]{1,0,3,2:T(2,128)}, f32[2,64,18,1]{1,0,3,2:T(2,128)S(1)}, u32[]{:S(2)}, u32[]{:S(2)}) collective-permute-start(f32[2,64,18,1]{1,0,3,2:T(2,128)} %copy.304), channel_id=1, source_target_pairs={{1,0},{2,1},{3,2},{5,4},{6,5},{7,6},{9,8},{10,9},{11,10},{13,12},{... | collective-permute-start | bytes 27656 | tf_op jit(solution)/shard_map/ppermute | solution.py:17
  17.6 7.0 %collective-permute-start.2 = (f32[2,64,18,1]{1,0,3,2:T(2,128)S(1)}, f32[2,64,18,1]{1,0,3,2:T(2,128)}, u32[]{:S(2)}, u32[]{:S(2)}) collective-permute-start(f32[2,64,18,1]{1,0,3,2:T(2,128)S(1)} %copy.303), channel_id=1, source_target_pairs={{0,1},{1,2},{2,3},{4,5},{5,6},{6,7},{8,9},{9,10},{10,11},{12,13},{... | collective-permute-start | bytes 27656 | tf_op jit(solution)/shard_map/ppermute | solution.py:14
  26.8 1.0 copy-start
  26.8 1.2 copy-start.19
  26.8 1.3 copy-start.20
  36.0 1.0 copy-start.10
  38.0 1.0 copy-start.1
  39.8 4.5 %copy-start.2 = (f32[64,16,128]{2,0,1:T(8,128)}, f32[64,16,128]{2,0,1:T(8,128)S(1)}, u32[]{:S(2)}) copy-start(f32[64,16,128]{2,0,1:T(8,128)S(1)} %get-tuple-element.745) | copy-start | bytes 1572868
  39.8 4.5 %copy-start.4 = (f32[64,16,128]{2,0,1:T(8,128)}, f32[64,16,128]{2,0,1:T(8,128)S(1)}, u32[]{:S(2)}) copy-start(f32[64,16,128]{2,0,1:T(8,128)S(1)} %get-tuple-element.747) | copy-start | bytes 1572868
  73.7 27.4 %copy-start.11 = (f32[64,16,128]{2,0,1:T(8,128)S(1)}, f32[64,16,128]{2,0,1:T(8,128)}, u32[]{:S(2)}) copy-start(f32[64,16,128]{2,0,1:T(8,128)} %copy-done.10) | copy-start | bytes 1572868
  74.4 26.7 %copy-start.9 = (f32[64,16,128]{2,0,1:T(8,128)S(1)}, f32[64,16,128]{2,0,1:T(8,128)}, u32[]{:S(2)}) copy-start(f32[64,16,128]{2,0,1:T(8,128)} %copy-done.8) | copy-start | bytes 1572868
  86.5 14.6 %copy-start.7 = (f32[64,16,128]{2,0,1:T(8,128)S(1)}, f32[64,16,128]{2,0,1:T(8,128)}, u32[]{:S(2)}) copy-start(f32[64,16,128]{2,0,1:T(8,128)} %copy-done.6) | copy-start | bytes 1572868
  101.1 1.0 copy-start.15
  101.1 1.2 copy-start.16
  101.1 1.3 copy-start.17
  101.1 1.5 %copy-start.18 = (f32[64,16,127]{2,0,1:T(8,128)S(1)}, f32[64,16,127]{2,0,1:T(8,128)}, u32[]{:S(2)}) copy-start(f32[64,16,127]{2,0,1:T(8,128)} %get-tuple-element.972) | copy-start | bytes 1560580
  101.2 1.5 %copy-start.3 = (f32[64,16,128]{2,0,1:T(8,128)S(1)}, f32[64,16,128]{2,0,1:T(8,128)}, u32[]{:S(2)}) copy-start(f32[64,16,128]{2,0,1:T(8,128)} %copy-done.2) | copy-start | bytes 1572868
  101.2 1.7 %copy-start.5 = (f32[64,16,128]{2,0,1:T(8,128)S(1)}, f32[64,16,128]{2,0,1:T(8,128)}, u32[]{:S(2)}) copy-start(f32[64,16,128]{2,0,1:T(8,128)} %copy-done.4) | copy-start | bytes 1572868
  101.3 1.8 %copy-start.13 = (f32[64,16,127]{2,0,1:T(8,128)S(1)}, f32[64,16,127]{2,0,1:T(8,128)}, u32[]{:S(2)}) copy-start(f32[64,16,127]{2,0,1:T(8,128)} %get-tuple-element.938) | copy-start | bytes 1560580
  101.3 2.0 %copy-start.14 = (f32[64,16,127]{2,0,1:T(8,128)S(1)}, f32[64,16,127]{2,0,1:T(8,128)}, u32[]{:S(2)}) copy-start(f32[64,16,127]{2,0,1:T(8,128)} %get-tuple-element.939) | copy-start | bytes 1560580
  121.5 14.4 %copy-start.12 = (f32[64,16,128]{2,1,0:T(8,128)S(1)}, f32[64,16,128]{2,1,0:T(8,128)}, u32[]{:S(2)}) copy-start(f32[64,16,128]{2,1,0:T(8,128)} %param.10) | copy-start | bytes 1572868
  (3 other events, 2.3 us)
Sparse Core Ops, SparseCore 0:
  37.9 31.1 all-gather.3
where the time goes:
time: 146 us; the launch traced here: 144 us
  other arithmetic  43.1 us (30%)
  local copies, waits for them, and re-layouts  36.4 us (25%)
  waiting for transfers between devices  24.6 us (17%)
  between operations  14.2 us (10%)
  blocking collectives  13.8 us (9%)
  starting transfers between devices  11.8 us (8%)
    dynamic_update_slice x24, other arithmetic, join_spikes(): unused, outputs = lax.scan(forward, (zero_plane, zero_plane), columns_in)  23.8 us
    all_gather x1, waiting for transfers between devices, on_device(): gathered = lax.all_gather(planes, 'row', axis=0, tiled=True)  23.3 us
    all_gather x1, blocking collectives, on_device(): gathered = lax.all_gather(planes, 'col', axis=0, tiled=True)  13.8 us
    add x11, other arithmetic, reduce_lines(): column + left_factor * shifted(column, line_axis, stride, 0.0)  10.7 us
    slice x41, local copies, waits for them, and re-layouts, shifted(): kept_part = lax.slice_in_dim(values, 0, length - stride, axis=line_axis)  9.44 us
    ppermute x2, starting transfers between devices, padded_2(): lax.ppermute(lax.slice_in_dim(block, block.shape[dim] - width, None, axis...  9.22 us
    unnamed x55, local copies, waits for them, and re-layouts  8.25 us
    slice x24, local copies, waits for them, and re-layouts, shifted(): kept_part = lax.slice_in_dim(values, -stride, length, axis=line_axis)  5.6 us
  transfers between devices with their start and end apart: 5, of which 3 were waited for; matrix products, arithmetic and copies ran while one was open for 6% of the time, Pallas kernels for 0%

commit v1 on v0

v1 whole, which is shorter than its diff:
```python
import functools

import jax
import jax.numpy as jnp
from jax import lax
from jax.experimental import pallas as pl
from jax.experimental.pallas import tpu as pltpu
from jax.sharding import PartitionSpec as P

MESH = pl.DeviceIdType.MESH
z_weight = 0.02
LANES = 128
UNROLL = 8


def send_all(axis, count, source_of, target, send_sems, recv_sems):
    me = lax.axis_index(axis)
    copies = []
    for step in range(1, count):
        peer = lax.rem(me + step, count)
        copy = pltpu.make_async_remote_copy(
            src_ref=source_of(peer),
            dst_ref=target.at[me],
            send_sem=send_sems.at[step],
            recv_sem=recv_sems.at[step],
            device_id={axis: peer},
            device_id_type=MESH,
        )
        copy.start()
        copies.append(copy)
    return copies


def factor_faces(mats, count):
    rows = []
    h_prev = None
    for m in range(count - 1):
        face = 0.5 * (mats(m, 4) + mats(m + 1, 3))
        pivot = 1.0 / face + mats(m + 1, 0) + mats(m, 2)
        if m > 0:
            pivot = pivot - mats(m, 1) * h_prev
        inverse = 1.0 / pivot
        h_prev = mats(m + 1, 1) * inverse
        rows.append((inverse, h_prev))
    return rows


def solve_faces(rows, mats, values, count):
    partial = []
    for m in range(count - 1):
        right = values(m + 1, 0) - values(m, 1)
        if m > 0:
            right = right + mats(m, 1) * partial[-1]
        partial.append(right * rows[m][0])
    fluxes = [None] * (count - 1)
    for m in reversed(range(count - 1)):
        fluxes[m] = partial[m]
        if m < count - 2:
            fluxes[m] = fluxes[m] + rows[m][1] * fluxes[m + 1]
    return fluxes


def kernel(
    dims, field_hbm, cond_hbm, out_ref,
    fbuf, cbuf, xu, xk, xr, xinv, xw, xb, kt, yr, yinv, yw, dt,
    pack, pack_l, pack_r, xm, xm_in, xv, xv_in, xj, xj_in, ym_in, yv_in, ym, yv,
    in_sems, halo_send, halo_recv, xm_send, xm_recv, xv_send, xv_recv, xj_send, xj_recv,
    ym_send, ym_recv, yv_send, yv_recv,
):
    n_row, n_col, nz, nx, ny = dims
    zs = nz // n_row
    blocks = nz * nx // LANES
    row = lax.axis_index("row")
    col = lax.axis_index("col")
    load_c = pltpu.make_async_copy(cond_hbm, cbuf.at[pl.ds(nx, nz * nx)], in_sems.at[0])
    load_f = pltpu.make_async_copy(field_hbm, fbuf.at[pl.ds(nx, nz * nx)], in_sems.at[1])
    load_c.start()
    load_f.start()
    barrier = pltpu.get_barrier_semaphore()
    for step in range(1, n_row):
        pl.semaphore_signal(
            barrier, inc=1, device_id={"row": lax.rem(row + step, n_row)}, device_id_type=MESH
        )
    for step in range(1, n_col):
        pl.semaphore_signal(
            barrier, inc=1, device_id={"col": lax.rem(col + step, n_col)}, device_id_type=MESH
        )
    edge = jnp.zeros((nx, ny), jnp.float32)
    for buf in (fbuf, cbuf):
        buf[pl.ds(0, nx), :] = edge
        buf[pl.ds((nz + 1) * nx, nx), :] = edge

    @pl.when(col == 0)
    def _():
        pack_l[...] = jnp.zeros_like(pack_l)

    @pl.when(col == n_col - 1)
    def _():
        pack_r[...] = jnp.zeros_like(pack_r)

    load_c.wait()
    load_f.wait()

    lane = lax.broadcasted_iota(jnp.int32, (nz, ny), 1)
    pair = lane // 2
    packed = jnp.zeros((nz, ny), jnp.float32)
    for x in range(nx):
        u = fbuf[pl.ds(nx + x, nz, stride=nx), :]
        k = cbuf[pl.ds(nx + x, nz, stride=nx), :]
        xu[x] = u
        xk[x] = k
        packed = jnp.where(pair == x, pltpu.roll(u, 2 * x + 1, 1), packed)
        packed = jnp.where(pair == nx + x, pltpu.roll(k, 2 * (nx + x) + 1, 1), packed)
    pack[...] = packed
    pl.semaphore_wait(barrier, n_row + n_col - 2)

    to_right = pltpu.make_async_remote_copy(
        src_ref=pack, dst_ref=pack_l, send_sem=halo_send.at[0], recv_sem=halo_recv.at[0],
        device_id={"col": jnp.minimum(col + 1, n_col - 1)}, device_id_type=MESH,
    )
    to_left = pltpu.make_async_remote_copy(
        src_ref=pack, dst_ref=pack_r, send_sem=halo_send.at[1], recv_sem=halo_recv.at[1],
        device_id={"col": jnp.maximum(col - 1, 0)}, device_id_type=MESH,
    )

    @pl.when(col < n_col - 1)
    def _():
        to_right.start()

    @pl.when(col > 0)
    def _():
        to_left.start()

    first_x = jnp.where(row == 0, 0.5, 0.0).astype(jnp.float32)
    last_x = jnp.where(row == n_row - 1, 0.5, 0.0).astype(jnp.float32)
    first_y = jnp.where(col == 0, 0.5, 0.0).astype(jnp.float32)
    last_y = jnp.where(col == n_col - 1, 0.5, 0.0).astype(jnp.float32)
    s = 1.0 + first_x * xk[0]
    prod = jnp.ones((nz, ny), jnp.float32)
    gff = jnp.zeros((nz, ny), jnp.float32)
    for x in range(nx):
        if x < nx - 1:
            e = 0.5 * (xk[x] + xk[x + 1])
            inv = 1.0 / (s + e)
            ratio = e * inv
            xr[x] = ratio
        else:
            inv = 1.0 / (s + last_x * xk[x])
        weight = prod * inv
        xinv[x] = inv
        xw[x] = weight
        gff = gff + prod * weight
        if x < nx - 1:
            prod = prod * ratio
            s = 1.0 + s * ratio
    for q, value in enumerate((gff, weight, inv, xk[0], xk[nx - 1])):
        for j in range(n_row):
            xm[j, q] = value[j * zs : (j + 1) * zs]
    xm_copies = send_all("row", n_row, lambda peer: xm.at[peer], xm_in, xm_send, xm_recv)
    xm_in[row] = xm[row]

    below = first_x * xk[0] * xu[0]
    for x in range(nx):
        u = xu[x]
        k = xk[x]
        flux = 0.5 * (k + pltpu.roll(k, ny - 1, 1)) * (pltpu.roll(u, ny - 1, 1) - u)
        flux = jnp.where(lane == ny - 1, 0.0, flux)
        total = flux - pltpu.roll(flux, 1, 1)
        k_up = cbuf[pl.ds(2 * nx + x, nz, stride=nx), :]
        u_up = fbuf[pl.ds(2 * nx + x, nz, stride=nx), :]
        k_down = cbuf[pl.ds(x, nz, stride=nx), :]
        u_down = fbuf[pl.ds(x, nz, stride=nx), :]
        total = total + 0.5 * z_weight * ((k + k_up) * (u_up - u) - (k + k_down) * (u - u_down))
        if x < nx - 1:
            above = 0.5 * (k + xk[x + 1]) * (xu[x + 1] - u)
        else:
            above = -last_x * k * u
        xb[x] = total + (above - below)
        below = above

    for p in range(blocks):
        per = LANES // nz
        tile = jnp.concatenate([xk[p * per + i] for i in range(per)], axis=0)
        kt[pl.ds(p, ny, stride=blocks), :] = tile.T

    @pl.when(col > 0)
    def _():
        to_right.wait_recv()

    @pl.when(col < n_col - 1)
    def _():
        to_left.wait_recv()

    other = jnp.where(
        lane % 2 == 0, pltpu.roll(pack_r[...], ny - 1, 1), pltpu.roll(pack_l[...], 1, 1)
    )
    mine = pack[...]
    k_sum = pltpu.roll(mine + other, ny - 2 * nx, 1)
    outer = 0.5 * k_sum * (other - mine)
    ends = (lane == 0) | (lane == ny - 1)

    value = None
    for x in range(nx):
        here = xb[x] + jnp.where(ends, pltpu.roll(outer, ny - 1 - 2 * x, 1), 0.0)
        value = here if x == 0 else here + xr[x - 1] * value
        xb[x] = value
        free_first = xw[x] * value if x == 0 else free_first + xw[x] * value
    free_last = xinv[nx - 1] * value
    for q, v in enumerate((xu[0] + free_first, xu[nx - 1] + free_last)):
        for j in range(n_row):
            xv[j, q] = v[j * zs : (j + 1) * zs]
    xv_copies = send_all("row", n_row, lambda peer: xv.at[peer], xv_in, xv_send, xv_recv)
    xv_in[row] = xv[row]

    def y_at(y):
        if isinstance(y, int):
            return pl.ds(y * blocks, blocks)
        return pl.ds(pl.multiple_of(y * blocks, blocks), blocks)

    def y_factor(y, state):
        k, s, prod, gff = state
        k_next = kt[y_at(y + 1), :]
        e = 0.5 * (k + k_next)
        inv = 1.0 / (s + e)
        ratio = e * inv
        weight = prod * inv
        yr[y_at(y), :] = ratio
        yinv[y_at(y), :] = inv
        yw[y_at(y), :] = weight
        return k_next, 1.0 + s * ratio, prod * ratio, gff + prod * weight

    def unrolled(step, base, state):
        for i in range(UNROLL):
            state = step(base * UNROLL + i, state)
        return state

    trips = ny // UNROLL
    k_first = kt[y_at(0), :]
    one = jnp.ones_like(k_first)
    state = (k_first, 1.0 + first_y * k_first, one, jnp.zeros_like(one))
    state = lax.fori_loop(0, trips - 1, lambda t, c: unrolled(y_factor, t, c), state)
    for y in range((trips - 1) * UNROLL, ny - 1):
        state = y_factor(y, state)
    k_last, s, prod, gff = state
    inv = 1.0 / (s + last_y * k_last)
    weight = prod * inv
    gff = gff + prod * weight
    yinv[y_at(ny - 1), :] = inv
    yw[y_at(ny - 1), :] = weight
    for q, v in enumerate((gff, weight, inv, k_first, k_last)):
        ym[q] = v
    ym_copies = send_all("col", n_col, lambda peer: ym, ym_in, ym_send, ym_recv)
    ym_in[col] = ym[...]

    for copy in xm_copies:
        copy.wait_recv()
    x_mats = lambda m, q: xm_in[m, q]
    x_rows = factor_faces(x_mats, n_row)
    for copy in xv_copies:
        copy.wait_recv()
    fluxes = solve_faces(x_rows, x_mats, lambda m, q: xv_in[m, q], n_row)
    nothing = jnp.zeros((zs, ny), jnp.float32)
    for m in range(n_row):
        xj[m, 0] = fluxes[m - 1] if m > 0 else nothing
        xj[m, 1] = fluxes[m] if m < n_row - 1 else nothing
    xj_copies = send_all("row", n_row, lambda peer: xj.at[peer], xj_in, xj_send, xj_recv)
    xj_in[row] = xj[row]

    for copy in ym_copies:
        copy.wait_recv()
    y_mats = lambda m, q: ym_in[m, q]
    y_rows = factor_faces(y_mats, n_col)
    for copy in xj_copies:
        copy.wait_recv()

    enter = jnp.concatenate([xj_in[j, 0] for j in range(n_row)], axis=0)
    leave = jnp.concatenate([xj_in[j, 1] for j in range(n_row)], axis=0)
    for x in reversed(range(nx)):
        if x == nx - 1:
            delta = (xb[x] + leave) * xinv[x] - enter * xw[x]
        else:
            delta = xb[x] * xinv[x] - enter * xw[x] + xr[x] * delta
        xb[x] = delta
    for p in range(blocks):
        tile = jnp.concatenate([xb[p * per + i] for i in range(per)], axis=0)
        dt[pl.ds(p, ny, stride=blocks), :] = tile.T

    def y_forward(y, state):
        value, free_first = state
        value = dt[y_at(y), :] + yr[y_at(y - 1), :] * value
        dt[y_at(y), :] = value
        return value, free_first + yw[y_at(y), :] * value

    value = dt[y_at(0), :]
    state = (value, yw[y_at(0), :] * value)
    for y in range(1, UNROLL):
        state = y_forward(y, state)
    value, free_first = lax.fori_loop(1, trips, lambda t, c: unrolled(y_forward, t, c), state)
    yv[0] = free_first
    yv[1] = yinv[y_at(ny - 1), :] * value
    yv_copies = send_all("col", n_col, lambda peer: yv, yv_in, yv_send, yv_recv)
    yv_in[col] = yv[...]
    for copy in yv_copies:
        copy.wait_recv()
    fluxes = solve_faces(y_rows, y_mats, lambda m, q: yv_in[m, q], n_col)
    enter = jnp.zeros_like(one)
    leave = jnp.zeros_like(one)
    for m in range(n_col - 1):
        enter = jnp.where(col == m + 1, fluxes[m], enter)
        leave = jnp.where(col == m, fluxes[m], leave)

    def y_backward(y, delta):
        free = dt[y_at(y), :] * yinv[y_at(y), :] - enter * yw[y_at(y), :]
        delta = free + yr[y_at(y), :] * delta
        dt[y_at(y), :] = delta
        return delta

    def y_backward_trip(t, delta):
        top = ny - 1 - t * UNROLL
        for i in range(UNROLL):
            delta = y_backward(top - i, delta)
        return delta

    delta = (value + leave) * yinv[y_at(ny - 1), :] - enter * yw[y_at(ny - 1), :]
    dt[y_at(ny - 1), :] = delta
    for y in reversed(range(ny - UNROLL, ny - 1)):
        delta = y_backward(y, delta)
    lax.fori_loop(1, trips, y_backward_trip, delta)
    for p in range(blocks):
        tile = dt[pl.ds(p, ny, stride=blocks), :].T
        for i in range(per):
            x = p * per + i
            out_ref[pl.ds(x, nz, stride=nx), :] = tile[i * nz : (i + 1) * nz]

    @pl.when(col < n_col - 1)
    def _():
        to_right.wait_send()

    @pl.when(col > 0)
    def _():
        to_left.wait_send()

    for copies in (xm_copies, xv_copies, xj_copies, ym_copies, yv_copies):
        for copy in copies:
            copy.wait_send()


def solution(mesh):
    n_row, n_col = mesh.shape["row"], mesh.shape["col"]

    def on_device(field, conductivity):
        nz, nx, ny = field.shape
        zs = nz // n_row
        blocks = nz * nx // LANES
        flat = (nz * nx, ny)
        tall = pltpu.VMEM(((nz + 2) * nx, ny), jnp.float32)
        cube = pltpu.VMEM((nx, nz, ny), jnp.float32)
        lines = pltpu.VMEM((ny * blocks, LANES), jnp.float32)
        plane = pltpu.VMEM((nz, ny), jnp.float32)
        part = lambda count: pltpu.VMEM((n_row, count, zs, ny), jnp.float32)
        whole = lambda *lead: pltpu.VMEM((*lead, blocks, LANES), jnp.float32)
        sems = lambda count: pltpu.SemaphoreType.DMA((count,))
        delta = pl.pallas_call(
            functools.partial(kernel, (n_row, n_col, nz, nx, ny)),
            out_shape=jax.ShapeDtypeStruct(flat, jnp.float32),
            in_specs=[pl.BlockSpec(memory_space=pl.ANY)] * 2,
            out_specs=pl.BlockSpec(memory_space=pltpu.VMEM),
            scratch_shapes=[
                tall, tall, cube, cube, cube, cube, cube, cube,
                lines, lines, lines, lines, lines,
                plane, plane, plane,
                part(5), part(5), part(2), part(2), part(2), part(2),
                whole(n_col, 5), whole(n_col, 2), whole(5), whole(2),
                sems(2), sems(2), sems(2),
                *[sems(n_row)] * 6,
                *[sems(n_col)] * 4,
            ],
            compiler_params=pltpu.CompilerParams(
                collective_id=0, has_side_effects=True, vmem_limit_bytes=32 * 1024 * 1024
            ),
            name="adi_step",
        )(field.reshape(flat), conductivity.reshape(flat))
        return field + delta.reshape(field.shape)

    spec = P(None, "row", "col")
    return jax.shard_map(
        on_device, mesh=mesh, in_specs=(spec, spec), out_specs=spec, check_vma=False
    )
```

time: 146 us -> 23.8 us (0.16); the launches traced: 144 us -> 23.6 us
  other arithmetic: 43.1 us -> 0.86 us
  local copies, waits for them, and re-layouts: 36.4 us -> 2.08 us
  waiting for transfers between devices: 24.6 us -> 0 us
  Pallas kernels: 0 us -> 20.7 us
  between operations: 14.2 us -> 0.01 us
  blocking collectives: 13.8 us -> 0 us
  starting transfers between devices: 11.8 us -> 0 us
    dynamic_update_slice x24 -> x0, other arithmetic: 23.8 us -> none  [join_spikes(): unused, outputs = lax.scan(forward, (zero_plane, zero_plane), columns_in)]
    all_gather x1 -> x0, waiting for transfers between devices: 23.3 us -> none  [on_device(): gathered = lax.all_gather(planes, 'row', axis=0, tiled=True)]
    pallas_call x0 -> x1, Pallas kernels: none -> 20.7 us  [on_device(): pl.pallas_call(functools.partial(kernel, (n_row, n_col, nz, nx, ny)), out...]
    slice x71 -> x0, local copies, waits for them, and re-layouts: 18.5 us -> none  [the longest x41 9.44 us: shifted(): kept_part = lax.slice_in_dim(values, 0, length - stride, axis=line_axis)]
    all_gather x1 -> x0, blocking collectives: 13.8 us -> none  [on_device(): gathered = lax.all_gather(planes, 'col', axis=0, tiled=True)]
    add x19 -> x1, other arithmetic: 12.9 us -> 0.86 us  [on_device(): return field + delta.reshape(field.shape)]
    ppermute x4 -> x0, starting transfers between devices: 11.8 us -> none  [the longest x2 9.22 us: padded_2(): lax.ppermute(lax.slice_in_dim(block, block.shape[dim] - width, None, axis...]
    unnamed x55 -> x4, local copies, waits for them, and re-layouts: 8.25 us -> 2.08 us
  transfers between devices with their start and end apart: 5 -> 0, of which waited for: 3 -> 0; matrix products, arithmetic and copies ran while one was open for 6% -> 0% of each run, Pallas kernels for 0% -> 0%
where the time goes in v1:
time: 23.8 us; the launch traced here: 23.6 us
  Pallas kernels  20.7 us (87%)
  local copies, waits for them, and re-layouts  2.08 us (9%)
  other arithmetic  0.86 us (4%)
    pallas_call x1, Pallas kernels, on_device(): pl.pallas_call(functools.partial(kernel, (n_row, n_col, nz, nx, ny)), out...  20.7 us
    unnamed x4, local copies, waits for them, and re-layouts  2.08 us
    add x1, other arithmetic, on_device(): return field + delta.reshape(field.shape)  0.86 us

profile of v1, /device:TPU:0, one launch (start us, length us, event | category | flops | bytes accessed | tf_op | source)
XLA Modules:
  0.0 23.6 jit_solution(911039880567550344)
XLA Ops:
  0.0 0.0 copy-start
  0.0 1.0 %copy-done = f32[64,16,128]{2,1,0:T(8,128)S(1)} copy-done((f32[64,16,128]{2,1,0:T(8,128)S(1)}, f32[64,16,128]{2,1,0:T(8,128)}, u32[]{:S(2)}) %copy-start) | copy-done | bytes 524312
  1.0 0.0 copy-start.1
  1.0 1.0 %copy-done.1 = f32[64,16,128]{2,1,0:T(8,128)S(1)} copy-done((f32[64,16,128]{2,1,0:T(8,128)S(1)}, f32[64,16,128]{2,1,0:T(8,128)}, u32[]{:S(2)}) %copy-start.1) | copy-done | bytes 524312
  2.1 20.7 %adi_step.1 = f32[1024,128]{1,0:T(8,128)S(1)} custom-call(f32[1024,128]{1,0:T(8,128)S(1)} %bitcast.3, f32[1024,128]{1,0:T(8,128)S(1)} %bitcast.5), custom_call_target="tpu_custom_call" | custom-call | tf_op jit(solution)/shard_map/adi_step/pallas_call | solution.py:363
  22.8 0.9 %add.3 = f32[64,16,128]{2,1,0:T(8,128)} add(f32[64,16,128]{2,1,0:T(8,128)S(1)} %copy-done, f32[64,16,128]{2,1,0:T(8,128)S(1)} %bitcast.4) | non-fusion elementwise | flops 131072 | bytes 1572864 | tf_op jit(solution)/shard_map/add | solution.py:383
Async XLA Ops:
  0.0 1.0 %copy-start = (f32[64,16,128]{2,1,0:T(8,128)S(1)}, f32[64,16,128]{2,1,0:T(8,128)}, u32[]{:S(2)}) copy-start(f32[64,16,128]{2,1,0:T(8,128)} %param.2) | copy-start | bytes 1572868
  1.0 1.0 %copy-start.1 = (f32[64,16,128]{2,1,0:T(8,128)S(1)}, f32[64,16,128]{2,1,0:T(8,128)}, u32[]{:S(2)}) copy-start(f32[64,16,128]{2,1,0:T(8,128)} %param.3) | copy-start | bytes 1572868

commit v2 on v1

--- a/solution.py
+++ b/solution.py
@@ -11,6 +11,7 @@
 z_weight = 0.02
 LANES = 128
 UNROLL = 8
+PAD = 8
 
 
 def send_all(axis, count, source_of, target, send_sems, recv_sems):
@@ -62,7 +63,7 @@
 
 def kernel(
     dims, field_hbm, cond_hbm, out_ref,
-    fbuf, cbuf, xu, xk, xr, xinv, xw, xb, kt, yr, yinv, yw, dt,
+    xu, xk, xr, xinv, xw, xb, kt, yr, yinv, yw, dt,
     pack, pack_l, pack_r, xm, xm_in, xv, xv_in, xj, xj_in, ym_in, yv_in, ym, yv,
     in_sems, halo_send, halo_recv, xm_send, xm_recv, xv_send, xv_recv, xj_send, xj_recv,
     ym_send, ym_recv, yv_send, yv_recv,
@@ -72,10 +73,15 @@
     blocks = nz * nx // LANES
     row = lax.axis_index("row")
     col = lax.axis_index("col")
-    load_c = pltpu.make_async_copy(cond_hbm, cbuf.at[pl.ds(nx, nz * nx)], in_sems.at[0])
-    load_f = pltpu.make_async_copy(field_hbm, fbuf.at[pl.ds(nx, nz * nx)], in_sems.at[1])
-    load_c.start()
-    load_f.start()
+    inner = pl.ds(PAD, nz)
+    loads = []
+    for x in range(nx):
+        for source, target, sem in ((cond_hbm, xk, 0), (field_hbm, xu, 1)):
+            load = pltpu.make_async_copy(
+                source.at[:, x, 0, :], target.at[x, inner, :], in_sems.at[sem, x]
+            )
+            load.start()
+            loads.append(load)
     barrier = pltpu.get_barrier_semaphore()
     for step in range(1, n_row):
         pl.semaphore_signal(
@@ -85,10 +91,12 @@
         pl.semaphore_signal(
             barrier, inc=1, device_id={"col": lax.rem(col + step, n_col)}, device_id_type=MESH
         )
-    edge = jnp.zeros((nx, ny), jnp.float32)
-    for buf in (fbuf, cbuf):
-        buf[pl.ds(0, nx), :] = edge
-        buf[pl.ds((nz + 1) * nx, nx), :] = edge
+    edge = jnp.zeros((nx, PAD, ny), jnp.float32)
+    for buf in (xu, xk):
+        buf[:, pl.ds(0, PAD), :] = edge
+        buf[:, pl.ds(PAD + nz, PAD), :] = edge
+    field = lambda x: xu[x, inner, :]
+    cond = lambda x: xk[x, inner, :]
 
     @pl.when(col == 0)
     def _():
@@ -97,18 +105,14 @@
     @pl.when(col == n_col - 1)
     def _():
         pack_r[...] = jnp.zeros_like(pack_r)
-
-    load_c.wait()
-    load_f.wait()
 
     lane = lax.broadcasted_iota(jnp.int32, (nz, ny), 1)
     pair = lane // 2
     packed = jnp.zeros((nz, ny), jnp.float32)
     for x in range(nx):
-        u = fbuf[pl.ds(nx + x, nz, stride=nx), :]
-        k = cbuf[pl.ds(nx + x, nz, stride=nx), :]
-        xu[x] = u
-        xk[x] = k
+        loads[2 * x].wait()
+        loads[2 * x + 1].wait()
+        u, k = field(x), cond(x)
         packed = jnp.where(pair == x, pltpu.roll(u, 2 * x + 1, 1), packed)
         packed = jnp.where(pair == nx + x, pltpu.roll(k, 2 * (nx + x) + 1, 1), packed)
     pack[...] = packed
@@ -135,17 +139,17 @@
     last_x = jnp.where(row == n_row - 1, 0.5, 0.0).astype(jnp.float32)
     first_y = jnp.where(col == 0, 0.5, 0.0).astype(jnp.float32)
     last_y = jnp.where(col == n_col - 1, 0.5, 0.0).astype(jnp.float32)
-    s = 1.0 + first_x * xk[0]
+    s = 1.0 + first_x * cond(0)
     prod = jnp.ones((nz, ny), jnp.float32)
     gff = jnp.zeros((nz, ny), jnp.float32)
     for x in range(nx):
         if x < nx - 1:
-            e = 0.5 * (xk[x] + xk[x + 1])
+            e = 0.5 * (cond(x) + cond(x + 1))
             inv = 1.0 / (s + e)
             ratio = e * inv
             xr[x] = ratio
         else:
-            inv = 1.0 / (s + last_x * xk[x])
+            inv = 1.0 / (s + last_x * cond(x))
         weight = prod * inv
         xinv[x] = inv
         xw[x] = weight
@@ -153,26 +157,24 @@
         if x < nx - 1:
             prod = prod * ratio
             s = 1.0 + s * ratio
-    for q, value in enumerate((gff, weight, inv, xk[0], xk[nx - 1])):
+    for q, value in enumerate((gff, weight, inv, cond(0), cond(nx - 1))):
         for j in range(n_row):
             xm[j, q] = value[j * zs : (j + 1) * zs]
     xm_copies = send_all("row", n_row, lambda peer: xm.at[peer], xm_in, xm_send, xm_recv)
     xm_in[row] = xm[row]
 
-    below = first_x * xk[0] * xu[0]
-    for x in range(nx):
-        u = xu[x]
-        k = xk[x]
+    below = first_x * cond(0) * field(0)
+    for x in range(nx):
+        u = field(x)
+        k = cond(x)
         flux = 0.5 * (k + pltpu.roll(k, ny - 1, 1)) * (pltpu.roll(u, ny - 1, 1) - u)
         flux = jnp.where(lane == ny - 1, 0.0, flux)
         total = flux - pltpu.roll(flux, 1, 1)
-        k_up = cbuf[pl.ds(2 * nx + x, nz, stride=nx), :]
-        u_up = fbuf[pl.ds(2 * nx + x, nz, stride=nx), :]
-        k_down = cbuf[pl.ds(x, nz, stride=nx), :]
-        u_down = fbuf[pl.ds(x, nz, stride=nx), :]
+        k_up, u_up = xk[x, pl.ds(PAD + 1, nz), :], xu[x, pl.ds(PAD + 1, nz), :]
+        k_down, u_down = xk[x, pl.ds(PAD - 1, nz), :], xu[x, pl.ds(PAD - 1, nz), :]
         total = total + 0.5 * z_weight * ((k + k_up) * (u_up - u) - (k + k_down) * (u - u_down))
         if x < nx - 1:
-            above = 0.5 * (k + xk[x + 1]) * (xu[x + 1] - u)
+            above = 0.5 * (k + cond(x + 1)) * (field(x + 1) - u)
         else:
             above = -last_x * k * u
         xb[x] = total + (above - below)
@@ -180,7 +182,7 @@
 
     for p in range(blocks):
         per = LANES // nz
-        tile = jnp.concatenate([xk[p * per + i] for i in range(per)], axis=0)
+        tile = jnp.concatenate([cond(p * per + i) for i in range(per)], axis=0)
         kt[pl.ds(p, ny, stride=blocks), :] = tile.T
 
     @pl.when(col > 0)
@@ -206,7 +208,7 @@
         xb[x] = value
         free_first = xw[x] * value if x == 0 else free_first + xw[x] * value
     free_last = xinv[nx - 1] * value
-    for q, v in enumerate((xu[0] + free_first, xu[nx - 1] + free_last)):
+    for q, v in enumerate((field(0) + free_first, field(nx - 1) + free_last)):
         for j in range(n_row):
             xv[j, q] = v[j * zs : (j + 1) * zs]
     xv_copies = send_all("row", n_row, lambda peer: xv.at[peer], xv_in, xv_send, xv_recv)
@@ -330,7 +332,7 @@
         tile = dt[pl.ds(p, ny, stride=blocks), :].T
         for i in range(per):
             x = p * per + i
-            out_ref[pl.ds(x, nz, stride=nx), :] = tile[i * nz : (i + 1) * nz]
+            out_ref[pl.ds(x, nz, stride=nx), :] = field(x) + tile[i * nz : (i + 1) * nz]
 
     @pl.when(col < n_col - 1)
     def _():
@@ -353,25 +355,26 @@
         zs = nz // n_row
         blocks = nz * nx // LANES
         flat = (nz * nx, ny)
-        tall = pltpu.VMEM(((nz + 2) * nx, ny), jnp.float32)
+        tall = pltpu.VMEM((nx, nz + 2 * PAD, ny), jnp.float32)
         cube = pltpu.VMEM((nx, nz, ny), jnp.float32)
         lines = pltpu.VMEM((ny * blocks, LANES), jnp.float32)
         plane = pltpu.VMEM((nz, ny), jnp.float32)
         part = lambda count: pltpu.VMEM((n_row, count, zs, ny), jnp.float32)
         whole = lambda *lead: pltpu.VMEM((*lead, blocks, LANES), jnp.float32)
         sems = lambda count: pltpu.SemaphoreType.DMA((count,))
-        delta = pl.pallas_call(
+        rows = (nz, nx, 1, ny)
+        out = pl.pallas_call(
             functools.partial(kernel, (n_row, n_col, nz, nx, ny)),
             out_shape=jax.ShapeDtypeStruct(flat, jnp.float32),
-            in_specs=[pl.BlockSpec(memory_space=pl.ANY)] * 2,
+            in_specs=[pl.BlockSpec(memory_space=pltpu.HBM)] * 2,
             out_specs=pl.BlockSpec(memory_space=pltpu.VMEM),
             scratch_shapes=[
-                tall, tall, cube, cube, cube, cube, cube, cube,
+                tall, tall, cube, cube, cube, cube,
                 lines, lines, lines, lines, lines,
                 plane, plane, plane,
                 part(5), part(5), part(2), part(2), part(2), part(2),
                 whole(n_col, 5), whole(n_col, 2), whole(5), whole(2),
-                sems(2), sems(2), sems(2),
+                pltpu.SemaphoreType.DMA((2, nx)), sems(2), sems(2),
                 *[sems(n_row)] * 6,
                 *[sems(n_col)] * 4,
             ],
@@ -379,8 +382,11 @@
                 collective_id=0, has_side_effects=True, vmem_limit_bytes=32 * 1024 * 1024
             ),
             name="adi_step",
-        )(field.reshape(flat), conductivity.reshape(flat))
-        return field + delta.reshape(field.shape)
+        )(
+            pltpu.with_memory_space_constraint(field.reshape(rows), pltpu.HBM),
+            pltpu.with_memory_space_constraint(conductivity.reshape(rows), pltpu.HBM),
+        )
+        return out.reshape(field.shape)
 
     spec = P(None, "row", "col")
     return jax.shard_map(

time: 23.8 us -> 21.9 us (0.920)
  local copies, waits for them, and re-layouts: 2.08 us -> 0.8 us
  other arithmetic: 0.86 us -> 0 us
    unnamed x4 -> x1, local copies, waits for them, and re-layouts: 2.08 us -> 0.8 us
    add x1 -> x0, other arithmetic: 0.86 us -> none  [on_device(): return field + delta.reshape(field.shape)]
    pallas_call x1, Pallas kernels: 20.7 us -> 20.9 us  [on_device(): pl.pallas_call(functools.partial(kernel, (n_row, n_col, nz, nx, ny)), out...]
where the time goes in v2:
time: 21.9 us; the launch traced here: 21.7 us
  Pallas kernels  20.9 us (95%)
  local copies, waits for them, and re-layouts  0.8 us (4%)
    pallas_call x1, Pallas kernels, on_device(): pl.pallas_call(functools.partial(kernel, (n_row, n_col, nz, nx, ny)), out...  20.9 us
    unnamed x1, local copies, waits for them, and re-layouts  0.8 us

profile of v2, /device:TPU:0, one launch (start us, length us, event | category | flops | bytes accessed | tf_op | source)
XLA Modules:
  0.0 21.7 jit_solution(17850712054022185892)
XLA Ops:
  0.0 20.9 %adi_step.1 = f32[1024,128]{1,0:T(8,128)S(1)} custom-call(f32[64,16,1,128]{3,2,1,0:T(1,128)} %bitcast.4, f32[64,16,1,128]{3,2,1,0:T(1,128)} %bitcast.5), custom_call_target="tpu_custom_call" | custom-call | tf_op jit(solution)/shard_map/adi_step/pallas_call | solution.py:366
  20.9 0.8 %copy.4 = f32[64,16,128]{2,1,0:T(8,128)} copy(f32[64,16,128]{2,1,0:T(8,128)S(1)} %bitcast.3) | data formatting | bytes 1048576

commit v3 on v2

--- a/solution.py
+++ b/solution.py
@@ -12,6 +12,26 @@
 LANES = 128
 UNROLL = 8
 PAD = 8
+PITCH_PAD = 8
+
+
+def row_groups(count):
+    every = range(1, count)
+    if count < 8 or count & (count - 1):
+        return list(every), False
+    return [o for o in every if not (o & 2 and o >> 2)], True
+
+
+def flipped(index, offset, count):
+    if count & (count - 1):
+        return lax.rem(index + offset, count)
+    result = index
+    bit = 1
+    while bit <= offset:
+        if offset & bit:
+            result = result + bit * (1 - 2 * ((index // bit) % 2))
+        bit *= 2
+    return result
 
 
 def send_all(axis, count, source_of, target, send_sems, recv_sems):
@@ -63,10 +83,10 @@
 
 def kernel(
     dims, field_hbm, cond_hbm, out_ref,
-    xu, xk, xr, xinv, xw, xb, kt, yr, yinv, yw, dt,
+    zu, zk, xu, xk, xr, xinv, xw, xb, kt, yr, yinv, yw, dt,
     pack, pack_l, pack_r, xm, xm_in, xv, xv_in, xj, xj_in, ym_in, yv_in, ym, yv,
     in_sems, halo_send, halo_recv, xm_send, xm_recv, xv_send, xv_recv, xj_send, xj_recv,
-    ym_send, ym_recv, yv_send, yv_recv,
+    ym_send, ym_recv, yv_send, yv_recv, row_token, col_token,
 ):
     n_row, n_col, nz, nx, ny = dims
     zs = nz // n_row
@@ -75,22 +95,27 @@
     col = lax.axis_index("col")
     inner = pl.ds(PAD, nz)
     loads = []
-    for x in range(nx):
-        for source, target, sem in ((cond_hbm, xk, 0), (field_hbm, xu, 1)):
-            load = pltpu.make_async_copy(
-                source.at[:, x, 0, :], target.at[x, inner, :], in_sems.at[sem, x]
-            )
-            load.start()
-            loads.append(load)
+    for source, target, sem in ((field_hbm, zu, 0), (cond_hbm, zk, 1)):
+        load = pltpu.make_async_copy(
+            source, target.at[:, pl.ds(0, nx), :], in_sems.at[sem]
+        )
+        load.start()
+        loads.append(load)
     barrier = pltpu.get_barrier_semaphore()
-    for step in range(1, n_row):
+    near, relayed = row_groups(n_row)
+    for offset in near:
         pl.semaphore_signal(
-            barrier, inc=1, device_id={"row": lax.rem(row + step, n_row)}, device_id_type=MESH
+            barrier, inc=1, device_id={"row": flipped(row, offset, n_row)}, device_id_type=MESH
         )
-    for step in range(1, n_col):
-        pl.semaphore_signal(
-            barrier, inc=1, device_id={"col": lax.rem(col + step, n_col)}, device_id_type=MESH
-        )
+
+    @pl.when(col < n_col - 1)
+    def _():
+        pl.semaphore_signal(barrier, inc=1, device_id={"col": col + 1}, device_id_type=MESH)
+
+    @pl.when(col > 0)
+    def _():
+        pl.semaphore_signal(barrier, inc=1, device_id={"col": col - 1}, device_id_type=MESH)
+
     edge = jnp.zeros((nx, PAD, ny), jnp.float32)
     for buf in (xu, xk):
         buf[:, pl.ds(0, PAD), :] = edge
@@ -109,14 +134,20 @@
     lane = lax.broadcasted_iota(jnp.int32, (nz, ny), 1)
     pair = lane // 2
     packed = jnp.zeros((nz, ny), jnp.float32)
-    for x in range(nx):
-        loads[2 * x].wait()
-        loads[2 * x + 1].wait()
-        u, k = field(x), cond(x)
-        packed = jnp.where(pair == x, pltpu.roll(u, 2 * x + 1, 1), packed)
-        packed = jnp.where(pair == nx + x, pltpu.roll(k, 2 * (nx + x) + 1, 1), packed)
-    pack[...] = packed
-    pl.semaphore_wait(barrier, n_row + n_col - 2)
+    pitch = nx + PITCH_PAD
+    for source, target, load, base in ((zu, xu, loads[0], 0), (zk, xk, loads[1], nx)):
+        load.wait()
+        flat = source.reshape(nz * pitch, ny)
+        for x in range(nx):
+            value = flat[pl.ds(x, nz, stride=pitch), :]
+            target[x, inner, :] = value
+            packed = jnp.where(pair == base + x, pltpu.roll(value, 2 * (base + x) + 1, 1), packed)
+    half = nz // 2
+    pack[...] = jnp.where(
+        lane[:half] < ny // 2, packed[:half], pltpu.roll(packed[half:], ny // 2, 1)
+    )
+    beside = jnp.minimum(col, 1) + jnp.minimum(n_col - 1 - col, 1)
+    pl.semaphore_wait(barrier, len(near) + beside)
 
     to_right = pltpu.make_async_remote_copy(
         src_ref=pack, dst_ref=pack_l, send_sem=halo_send.at[0], recv_sem=halo_recv.at[0],
@@ -134,6 +165,36 @@
     @pl.when(col > 0)
     def _():
         to_left.start()
+
+    if relayed:
+        pl.semaphore_signal(
+            row_token, inc=1, device_id={"row": flipped(row, 2, n_row)}, device_id_type=MESH
+        )
+
+    def pass_on(step):
+        @pl.when(col < n_col - 1)
+        def _():
+            pl.semaphore_signal(
+                col_token.at[0, step], inc=1, device_id={"col": col + 1}, device_id_type=MESH
+            )
+
+        @pl.when(col > 0)
+        def _():
+            pl.semaphore_signal(
+                col_token.at[1, step], inc=1, device_id={"col": col - 1}, device_id_type=MESH
+            )
+
+    def take_in(step):
+        @pl.when(col > 0)
+        def _():
+            pl.semaphore_wait(col_token.at[0, step], 1)
+
+        @pl.when(col < n_col - 1)
+        def _():
+            pl.semaphore_wait(col_token.at[1, step], 1)
+
+    if n_col > 2:
+        pass_on(0)
 
     first_x = jnp.where(row == 0, 0.5, 0.0).astype(jnp.float32)
     last_x = jnp.where(row == n_row - 1, 0.5, 0.0).astype(jnp.float32)
@@ -160,6 +221,8 @@
     for q, value in enumerate((gff, weight, inv, cond(0), cond(nx - 1))):
         for j in range(n_row):
             xm[j, q] = value[j * zs : (j + 1) * zs]
+    if relayed:
+        pl.semaphore_wait(row_token, 1)
     xm_copies = send_all("row", n_row, lambda peer: xm.at[peer], xm_in, xm_send, xm_recv)
     xm_in[row] = xm[row]
 
@@ -193,8 +256,12 @@
     def _():
         to_left.wait_recv()
 
+    for step in range(1, n_col - 2):
+        take_in(step - 1)
+        pass_on(step)
+    small = lax.broadcasted_iota(jnp.int32, (nz // 2, ny), 1)
     other = jnp.where(
-        lane % 2 == 0, pltpu.roll(pack_r[...], ny - 1, 1), pltpu.roll(pack_l[...], 1, 1)
+        small % 2 == 0, pltpu.roll(pack_r[...], ny - 1, 1), pltpu.roll(pack_l[...], 1, 1)
     )
     mine = pack[...]
     k_sum = pltpu.roll(mine + other, ny - 2 * nx, 1)
@@ -203,7 +270,9 @@
 
     value = None
     for x in range(nx):
-        here = xb[x] + jnp.where(ends, pltpu.roll(outer, ny - 1 - 2 * x, 1), 0.0)
+        place = ny - 1 - 2 * x
+        outer_x = (pltpu.roll(outer, place, 1), pltpu.roll(outer, place - ny // 2, 1))
+        here = xb[x] + jnp.where(ends, jnp.concatenate(outer_x, axis=0), 0.0)
         value = here if x == 0 else here + xr[x - 1] * value
         xb[x] = value
         free_first = xw[x] * value if x == 0 else free_first + xw[x] * value
@@ -251,6 +320,8 @@
     yw[y_at(ny - 1), :] = weight
     for q, v in enumerate((gff, weight, inv, k_first, k_last)):
         ym[q] = v
+    if n_col > 2:
+        take_in(n_col - 3)
     ym_copies = send_all("col", n_col, lambda peer: ym, ym_in, ym_send, ym_recv)
     ym_in[col] = ym[...]
 
@@ -356,35 +427,37 @@
         blocks = nz * nx // LANES
         flat = (nz * nx, ny)
         tall = pltpu.VMEM((nx, nz + 2 * PAD, ny), jnp.float32)
+        wide = pltpu.VMEM((nz, nx + PITCH_PAD, ny), jnp.float32)
         cube = pltpu.VMEM((nx, nz, ny), jnp.float32)
         lines = pltpu.VMEM((ny * blocks, LANES), jnp.float32)
-        plane = pltpu.VMEM((nz, ny), jnp.float32)
+        plane = pltpu.VMEM((nz // 2, ny), jnp.float32)
         part = lambda count: pltpu.VMEM((n_row, count, zs, ny), jnp.float32)
         whole = lambda *lead: pltpu.VMEM((*lead, blocks, LANES), jnp.float32)
         sems = lambda count: pltpu.SemaphoreType.DMA((count,))
-        rows = (nz, nx, 1, ny)
         out = pl.pallas_call(
             functools.partial(kernel, (n_row, n_col, nz, nx, ny)),
             out_shape=jax.ShapeDtypeStruct(flat, jnp.float32),
             in_specs=[pl.BlockSpec(memory_space=pltpu.HBM)] * 2,
             out_specs=pl.BlockSpec(memory_space=pltpu.VMEM),
             scratch_shapes=[
-                tall, tall, cube, cube, cube, cube,
+                wide, wide, tall, tall, cube, cube, cube, cube,
                 lines, lines, lines, lines, lines,
                 plane, plane, plane,
                 part(5), part(5), part(2), part(2), part(2), part(2),
                 whole(n_col, 5), whole(n_col, 2), whole(5), whole(2),
-                pltpu.SemaphoreType.DMA((2, nx)), sems(2), sems(2),
+                sems(2), sems(2), sems(2),
                 *[sems(n_row)] * 6,
                 *[sems(n_col)] * 4,
+                pltpu.SemaphoreType.REGULAR,
+                pltpu.SemaphoreType.REGULAR((2, n_col)),
             ],
             compiler_params=pltpu.CompilerParams(
                 collective_id=0, has_side_effects=True, vmem_limit_bytes=32 * 1024 * 1024
             ),
             name="adi_step",
         )(
-            pltpu.with_memory_space_constraint(field.reshape(rows), pltpu.HBM),
-            pltpu.with_memory_space_constraint(conductivity.reshape(rows), pltpu.HBM),
+            pltpu.with_memory_space_constraint(field, pltpu.HBM),
+            pltpu.with_memory_space_constraint(conductivity, pltpu.HBM),
         )
         return out.reshape(field.shape)
 

time: 21.9 us -> 21.2 us (0.968)
  Pallas kernels: 20.9 us -> 20.3 us
    pallas_call x1, Pallas kernels: 20.9 us -> 20.3 us  [on_device(): pl.pallas_call(functools.partial(kernel, (n_row, n_col, nz, nx, ny)), out...]
where the time goes in v3:
time: 21.2 us; the launch traced here: 21.1 us
  Pallas kernels  20.3 us (96%)
  local copies, waits for them, and re-layouts  0.8 us (4%)
    pallas_call x1, Pallas kernels, on_device(): pl.pallas_call(functools.partial(kernel, (n_row, n_col, nz, nx, ny)), out...  20.3 us
    unnamed x1, local copies, waits for them, and re-layouts  0.8 us

profile of v3, /device:TPU:0, one launch (start us, length us, event | category | flops | bytes accessed | tf_op | source)
XLA Modules:
  0.0 21.1 jit_solution(5648203545390297536)
XLA Ops:
  0.0 20.3 %adi_step.1 = f32[1024,128]{1,0:T(8,128)S(1)} custom-call(f32[64,16,128]{2,1,0:T(8,128)} %field_hbm.1, f32[64,16,128]{2,1,0:T(8,128)} %cond_hbm.1), custom_call_target="tpu_custom_call" | custom-call | tf_op jit(solution)/shard_map/adi_step/pallas_call | solution.py:437
  20.3 0.8 %copy.4 = f32[64,16,128]{2,1,0:T(8,128)} copy(f32[64,16,128]{2,1,0:T(8,128)S(1)} %bitcast.1) | data formatting | bytes 1048576

commit v4 on v3

--- a/solution.py
+++ b/solution.py
@@ -34,16 +34,16 @@
     return result
 
 
-def send_all(axis, count, source_of, target, send_sems, recv_sems):
+def send_all(axis, count, source_of, target, send_sems, recv_sems, offsets=None):
     me = lax.axis_index(axis)
     copies = []
-    for step in range(1, count):
-        peer = lax.rem(me + step, count)
+    for offset in offsets or range(count - 1, 0, -1):
+        peer = flipped(me, offset, count)
         copy = pltpu.make_async_remote_copy(
             src_ref=source_of(peer),
             dst_ref=target.at[me],
-            send_sem=send_sems.at[step],
-            recv_sem=recv_sems.at[step],
+            send_sem=send_sems.at[offset],
+            recv_sem=recv_sems.at[offset],
             device_id={axis: peer},
             device_id_type=MESH,
         )
@@ -146,56 +146,6 @@
     pack[...] = jnp.where(
         lane[:half] < ny // 2, packed[:half], pltpu.roll(packed[half:], ny // 2, 1)
     )
-    beside = jnp.minimum(col, 1) + jnp.minimum(n_col - 1 - col, 1)
-    pl.semaphore_wait(barrier, len(near) + beside)
-
-    to_right = pltpu.make_async_remote_copy(
-        src_ref=pack, dst_ref=pack_l, send_sem=halo_send.at[0], recv_sem=halo_recv.at[0],
-        device_id={"col": jnp.minimum(col + 1, n_col - 1)}, device_id_type=MESH,
-    )
-    to_left = pltpu.make_async_remote_copy(
-        src_ref=pack, dst_ref=pack_r, send_sem=halo_send.at[1], recv_sem=halo_recv.at[1],
-        device_id={"col": jnp.maximum(col - 1, 0)}, device_id_type=MESH,
-    )
-
-    @pl.when(col < n_col - 1)
-    def _():
-        to_right.start()
-
-    @pl.when(col > 0)
-    def _():
-        to_left.start()
-
-    if relayed:
-        pl.semaphore_signal(
-            row_token, inc=1, device_id={"row": flipped(row, 2, n_row)}, device_id_type=MESH
-        )
-
-    def pass_on(step):
-        @pl.when(col < n_col - 1)
-        def _():
-            pl.semaphore_signal(
-                col_token.at[0, step], inc=1, device_id={"col": col + 1}, device_id_type=MESH
-            )
-
-        @pl.when(col > 0)
-        def _():
-            pl.semaphore_signal(
-                col_token.at[1, step], inc=1, device_id={"col": col - 1}, device_id_type=MESH
-            )
-
-    def take_in(step):
-        @pl.when(col > 0)
-        def _():
-            pl.semaphore_wait(col_token.at[0, step], 1)
-
-        @pl.when(col < n_col - 1)
-        def _():
-            pl.semaphore_wait(col_token.at[1, step], 1)
-
-    if n_col > 2:
-        pass_on(0)
-
     first_x = jnp.where(row == 0, 0.5, 0.0).astype(jnp.float32)
     last_x = jnp.where(row == n_row - 1, 0.5, 0.0).astype(jnp.float32)
     first_y = jnp.where(col == 0, 0.5, 0.0).astype(jnp.float32)
@@ -221,11 +171,6 @@
     for q, value in enumerate((gff, weight, inv, cond(0), cond(nx - 1))):
         for j in range(n_row):
             xm[j, q] = value[j * zs : (j + 1) * zs]
-    if relayed:
-        pl.semaphore_wait(row_token, 1)
-    xm_copies = send_all("row", n_row, lambda peer: xm.at[peer], xm_in, xm_send, xm_recv)
-    xm_in[row] = xm[row]
-
     below = first_x * cond(0) * field(0)
     for x in range(nx):
         u = field(x)
@@ -243,45 +188,72 @@
         xb[x] = total + (above - below)
         below = above
 
+    beside = jnp.minimum(col, 1) + jnp.minimum(n_col - 1 - col, 1)
+    pl.semaphore_wait(barrier, len(near) + beside)
+
+    to_right = pltpu.make_async_remote_copy(
+        src_ref=pack, dst_ref=pack_l, send_sem=halo_send.at[0], recv_sem=halo_recv.at[0],
+        device_id={"col": jnp.minimum(col + 1, n_col - 1)}, device_id_type=MESH,
+    )
+    to_left = pltpu.make_async_remote_copy(
+        src_ref=pack, dst_ref=pack_r, send_sem=halo_send.at[1], recv_sem=halo_recv.at[1],
+        device_id={"col": jnp.maximum(col - 1, 0)}, device_id_type=MESH,
+    )
+
+    @pl.when(col < n_col - 1)
+    def _():
+        to_right.start()
+
+    @pl.when(col > 0)
+    def _():
+        to_left.start()
+
+    if relayed:
+        pl.semaphore_signal(
+            row_token, inc=1, device_id={"row": flipped(row, 2, n_row)}, device_id_type=MESH
+        )
+
+    def pass_on(step):
+        @pl.when(col < n_col - 1)
+        def _():
+            pl.semaphore_signal(
+                col_token.at[0, step], inc=1, device_id={"col": col + 1}, device_id_type=MESH
+            )
+
+        @pl.when(col > 0)
+        def _():
+            pl.semaphore_signal(
+                col_token.at[1, step], inc=1, device_id={"col": col - 1}, device_id_type=MESH
+            )
+
+    def take_in(step):
+        @pl.when(col > 0)
+        def _():
+            pl.semaphore_wait(col_token.at[0, step], 1)
+
+        @pl.when(col < n_col - 1)
+        def _():
+            pl.semaphore_wait(col_token.at[1, step], 1)
+
+    if n_col > 2:
+        pass_on(0)
+
+    xm_from = lambda peer: xm.at[peer]
+    xm_copies = send_all("row", n_row, xm_from, xm_in, xm_send, xm_recv, near)
+    xm_in[row] = xm[row]
+
     for p in range(blocks):
         per = LANES // nz
         tile = jnp.concatenate([cond(p * per + i) for i in range(per)], axis=0)
         kt[pl.ds(p, ny, stride=blocks), :] = tile.T
 
-    @pl.when(col > 0)
-    def _():
-        to_right.wait_recv()
-
-    @pl.when(col < n_col - 1)
-    def _():
-        to_left.wait_recv()
-
+    if relayed:
+        pl.semaphore_wait(row_token, 1)
+        far = [o for o in range(1, n_row) if o not in near]
+        xm_copies = xm_copies + send_all("row", n_row, xm_from, xm_in, xm_send, xm_recv, far)
     for step in range(1, n_col - 2):
         take_in(step - 1)
         pass_on(step)
-    small = lax.broadcasted_iota(jnp.int32, (nz // 2, ny), 1)
-    other = jnp.where(
-        small % 2 == 0, pltpu.roll(pack_r[...], ny - 1, 1), pltpu.roll(pack_l[...], 1, 1)
-    )
-    mine = pack[...]
-    k_sum = pltpu.roll(mine + other, ny - 2 * nx, 1)
-    outer = 0.5 * k_sum * (other - mine)
-    ends = (lane == 0) | (lane == ny - 1)
-
-    value = None
-    for x in range(nx):
-        place = ny - 1 - 2 * x
-        outer_x = (pltpu.roll(outer, place, 1), pltpu.roll(outer, place - ny // 2, 1))
-        here = xb[x] + jnp.where(ends, jnp.concatenate(outer_x, axis=0), 0.0)
-        value = here if x == 0 else here + xr[x - 1] * value
-        xb[x] = value
-        free_first = xw[x] * value if x == 0 else free_first + xw[x] * value
-    free_last = xinv[nx - 1] * value
-    for q, v in enumerate((field(0) + free_first, field(nx - 1) + free_last)):
-        for j in range(n_row):
-            xv[j, q] = v[j * zs : (j + 1) * zs]
-    xv_copies = send_all("row", n_row, lambda peer: xv.at[peer], xv_in, xv_send, xv_recv)
-    xv_in[row] = xv[row]
 
     def y_at(y):
         if isinstance(y, int):
@@ -324,6 +296,38 @@
         take_in(n_col - 3)
     ym_copies = send_all("col", n_col, lambda peer: ym, ym_in, ym_send, ym_recv)
     ym_in[col] = ym[...]
+
+    @pl.when(col > 0)
+    def _():
+        to_right.wait_recv()
+
+    @pl.when(col < n_col - 1)
+    def _():
+        to_left.wait_recv()
+
+    small = lax.broadcasted_iota(jnp.int32, (nz // 2, ny), 1)
+    other = jnp.where(
+        small % 2 == 0, pltpu.roll(pack_r[...], ny - 1, 1), pltpu.roll(pack_l[...], 1, 1)
+    )
+    mine = pack[...]
+    k_sum = pltpu.roll(mine + other, ny - 2 * nx, 1)
+    outer = 0.5 * k_sum * (other - mine)
+    ends = (lane == 0) | (lane == ny - 1)
+
+    value = None
+    for x in range(nx):
+        place = ny - 1 - 2 * x
+        outer_x = (pltpu.roll(outer, place, 1), pltpu.roll(outer, place - ny // 2, 1))
+        here = xb[x] + jnp.where(ends, jnp.concatenate(outer_x, axis=0), 0.0)
+        value = here if x == 0 else here + xr[x - 1] * value
+        xb[x] = value
+        free_first = xw[x] * value if x == 0 else free_first + xw[x] * value
+    free_last = xinv[nx - 1] * value
+    for q, v in enumerate((field(0) + free_first, field(nx - 1) + free_last)):
+        for j in range(n_row):
+            xv[j, q] = v[j * zs : (j + 1) * zs]
+    xv_copies = send_all("row", n_row, lambda peer: xv.at[peer], xv_in, xv_send, xv_recv)
+    xv_in[row] = xv[row]
 
     for copy in xm_copies:
         copy.wait_recv()

time: 21.2 us -> 22.6 us (1.066)
  Pallas kernels: 20.3 us -> 21.7 us
    pallas_call x1, Pallas kernels: 20.3 us -> 21.7 us  [on_device(): pl.pallas_call(functools.partial(kernel, (n_row, n_col, nz, nx, ny)), out...]
where the time goes in v4:
time: 22.6 us; the launch traced here: 22.5 us
  Pallas kernels  21.7 us (96%)
  local copies, waits for them, and re-layouts  0.8 us (4%)
    pallas_call x1, Pallas kernels, on_device(): pl.pallas_call(functools.partial(kernel, (n_row, n_col, nz, nx, ny)), out...  21.7 us
    unnamed x1, local copies, waits for them, and re-layouts  0.8 us

profile of v4, /device:TPU:0, one launch (start us, length us, event | category | flops | bytes accessed | tf_op | source)
XLA Modules:
  0.0 22.5 jit_solution(522991088381084399)
XLA Ops:
  0.0 21.7 %adi_step.1 = f32[1024,128]{1,0:T(8,128)S(1)} custom-call(f32[64,16,128]{2,1,0:T(8,128)} %field_hbm.1, f32[64,16,128]{2,1,0:T(8,128)} %cond_hbm.1), custom_call_target="tpu_custom_call" | custom-call | tf_op jit(solution)/shard_map/adi_step/pallas_call | solution.py:441
  21.7 0.8 %copy.4 = f32[64,16,128]{2,1,0:T(8,128)} copy(f32[64,16,128]{2,1,0:T(8,128)S(1)} %bitcast.1) | data formatting | bytes 1048576
